TPU v7x, 32 devices: a whole 2x2x4 slice. The times are simulated.
32 devices in a mesh: dp: 4 (over z), head: 8 (over y, x, core).
Axes of the slice: x: 2, y: 2, z: 4, core: 2. Of those that a mesh axis runs over, the one named last changes fastest.
Arguments:
- residual: float32 [96, 4096], P('dp', 'head'), parts along dimension 0, may hold values from -70 to 70
- norm_gain: float32 [4096], replicated, may hold values from 0.5 to 1.5
- w_query: bfloat16 [8, 256, 4096], P(None, 'head'), may hold values from -0.09375 to 0.09375
- w_key: bfloat16 [8, 256, 4096], P(None, 'head'), may hold values from -0.09375 to 0.09375
- w_value: bfloat16 [4096, 4096], P(None, 'head'), may hold values from -0.09375 to 0.09375
- w_gate: bfloat16 [4096, 4096], P(None, 'head'), may hold values from -0.09375 to 0.09375
- w_input: bfloat16 [8, 4096], replicated, may hold values from -0.09375 to 0.09375
- w_forget: bfloat16 [8, 4096], replicated, may hold values from -0.09375 to 0.09375
- b_input: float32 [8], replicated, may hold values from -2 to -0.5
- b_forget: float32 [8], replicated, may hold values from 0.5 to 4
- w_out: bfloat16 [4096, 4096], P('head'), may hold values from -0.125 to 0.125
- memory: bfloat16 [96, 8, 256, 512], P('dp', None, 'head'), parts along dimension 0, may hold values from -0.59765625 to 0.59765625
- normalizer: float32 [96, 8, 256], P('dp', None, 'head'), parts along dimension 0, may hold values from -0.6 to 0.6
- stabilizer: float32 [96, 8], P('dp'), parts along dimension 0, may hold values from -0.5 to 0.5
Outputs:
- res_out: float32 [96, 4096], P('dp', 'head'), parts along dimension 0
- mem_out: bfloat16 [96, 8, 256, 512], P('dp', None, 'head'), parts along dimension 0
- norm_out: float32 [96, 8, 256], P('dp', None, 'head'), parts along dimension 0
- stab_out: float32 [96, 8], P('dp'), parts along dimension 0
There are 4 independent parts, one for each index of `dp`. A program takes and returns all parts, laid end to end along the dimension named above; an argument that names none is the same for every part. Nothing has to cross between parts.
All inputs are finite; a program needn't handle non-finite values.
Results may differ from a plain program's by a relative error of at most 0.0095.
Values may be sent and summed in bfloat16 or wider, within the bound.
A program may use at most 64 MiB of HBM per device.

v0:
```python
import functools
import math

import jax
import jax.numpy as jnp
from jax import lax
from jax.experimental import pallas as pl
from jax.experimental.pallas import tpu as pltpu
from jax.sharding import PartitionSpec as P

GROUP = 8
LANES = 128
PIECES = 4
epsilon = 1e-06

NT = (((1,), (1,)), ((), ()))
NN = (((1,), (0,)), ((), ()))


def dot(a, b, dims=NN, precision=None):
    return lax.dot_general(a, b, dims, precision=precision, preferred_element_type=jnp.float32)


def kernel(
    n, batch, heads, rows, dv, width, key_scale,
    res_hbm, gain_hbm, wq_hbm, wk_hbm, wv_hbm, wg_hbm, wi_hbm, wf_hbm, bi_hbm, bf_hbm, wo_hbm, mem_hbm, nrm_hbm, stab_hbm,
    res_out, mem_out, nrm_out, stab_out,
    res, gain, wq, wk, wv, wg, wi, wf, bi, bf, wo, mem, nrm, stab,
    xs, sq, num_send, num_recv, den_send, den_recv, vals, out_send, out_recv,
    q_rows, n_rows, num_tile, val_rows, fcols, kcols,
    in_sem, mem_sem, x_send, x_recv, sq_send, sq_recv, num_ss, num_rs, den_ss, den_rs, val_ss, val_rs, out_ss, out_rs,
):
    me = lax.axis_index("head")
    groups = batch // GROUP
    hr = heads * rows
    share = n * width // heads
    barrier = pltpu.get_barrier_semaphore()

    def peer(d):
        return lax.rem(me + d, n)

    def source(d):
        return lax.rem(me + n - d, n)

    for d in range(1, n):
        pl.semaphore_signal(barrier, inc=1, device_id={"head": peer(d)}, device_id_type=pl.DeviceIdType.MESH)

    gain_part = gain_hbm.at[:, pl.ds(pl.multiple_of(me * width, width), width)]
    local = [
        (res_hbm, res), (gain_part, gain), (wq_hbm, wq), (wk_hbm, wk), (wi_hbm, wi), (wf_hbm, wf), (bi_hbm, bi), (bf_hbm, bf),
        (nrm_hbm, nrm), (stab_hbm, stab), (wv_hbm, wv), (wg_hbm, wg), (wo_hbm, wo),
    ]
    loads = [pltpu.make_async_copy(a, b, in_sem.at[i]) for i, (a, b) in enumerate(local)]
    (l_res, l_gain, l_wq, l_wk, l_wi, l_wf, l_bi, l_bf, l_nrm, l_stab, l_wv, l_wg, l_wo) = loads

    def mem_load(g):
        return pltpu.make_async_copy(
            mem_hbm.at[pl.ds(g * GROUP, GROUP)], mem.at[pl.ds(g * GROUP, GROUP)], mem_sem.at[g]
        )

    for copy in (l_res, l_gain, l_wq, l_wk):
        copy.start()
    for g in range(groups):
        mem_load(g).start()
    for copy in (l_wi, l_wf, l_bi, l_bf, l_nrm, l_stab, l_wv, l_wg, l_wo):
        copy.start()

    def remote(src, dst, ssem, rsem, target):
        return pltpu.make_async_remote_copy(
            src_ref=src, dst_ref=dst, send_sem=ssem, recv_sem=rsem,
            device_id={"head": target}, device_id_type=pl.DeviceIdType.MESH,
        )

    eye = lax.broadcasted_iota(jnp.int32, (batch, batch), 0) == lax.broadcasted_iota(jnp.int32, (batch, batch), 1)

    def to_row(col):
        return jnp.sum(jnp.where(eye, col, 0.0), axis=0, keepdims=True)

    def to_col(row):
        return jnp.sum(jnp.where(eye, row, 0.0), axis=1, keepdims=True)

    l_res.wait()
    l_gain.wait()
    own = res[...]
    xs[me] = (own * gain[...]).astype(jnp.bfloat16)
    sq[me] = jnp.zeros((1, LANES), jnp.float32)
    sq[me, :, 0:batch] = to_row(jnp.sum(own * own, axis=1, keepdims=True))
    den_send[...] = jnp.zeros_like(den_send)

    def x_copy(d, owner):
        return remote(xs.at[owner], xs.at[owner], x_send.at[d - 1], x_recv.at[d - 1], peer(d))

    def sq_copy(d, owner):
        return remote(sq.at[owner], sq.at[owner], sq_send.at[d - 1], sq_recv.at[d - 1], peer(d))

    def val_copy(d, owner):
        return remote(vals.at[owner], vals.at[owner], val_ss.at[d - 1], val_rs.at[d - 1], peer(d))

    def num_copy(d, g):
        return remote(num_send.at[peer(d), g], num_recv.at[d - 1, g], num_ss.at[d - 1, g], num_rs.at[d - 1, g], peer(d))

    def den_copy(d):
        head = lax.div(peer(d) * width, share)
        return remote(den_send.at[head], den_recv.at[d - 1], den_ss.at[d - 1], den_rs.at[d - 1], peer(d))

    def out_copy(d):
        return remote(out_send.at[d - 1], out_recv.at[d - 1], out_ss.at[d - 1], out_rs.at[d - 1], peer(d))

    pl.semaphore_wait(barrier, n - 1)
    for d in range(1, n):
        x_copy(d, me).start()
    for d in range(1, n):
        sq_copy(d, me).start()

    l_wq.wait()
    l_wk.wait()
    q_raw = jnp.zeros((batch, hr), jnp.float32)
    k_raw = jnp.zeros((batch, hr), jnp.float32)
    for d in range(n):
        owner = source(d)
        if d:
            x_copy(d, owner).wait_recv()
        cols = pl.ds(pl.multiple_of(owner * width, width), width)
        block = xs[owner]
        q_raw += dot(block, wq[:, cols], NT)
        k_raw += dot(block, wk[:, cols], NT)
    q_rows[...] = q_raw

    mine = lax.broadcasted_iota(jnp.int32, (heads, hr), 1) // rows == lax.broadcasted_iota(jnp.int32, (heads, hr), 0)

    def read_group(g, carry):
        mem_load(g).wait()
        block_q = q_rows[pl.ds(pl.multiple_of(g * GROUP, GROUP), GROUP), :]
        for j in range(GROUP):
            spread = jnp.where(mine, block_q[j : j + 1, :], 0.0)
            high = spread.astype(jnp.bfloat16)
            low = (spread - high.astype(jnp.float32)).astype(jnp.bfloat16)
            both = dot(jnp.concatenate([high, low], axis=0), mem[g * GROUP + j])
            num_tile[:, j, :] = both[:heads] + both[heads:]
        for p in range(n):
            head, col = p * width // dv, p * width % dv
            num_send[p, g] = num_tile[head, :, col : col + width].astype(jnp.bfloat16)
        for d in range(1, n):
            num_copy(d, g).start()
        return carry

    lax.fori_loop(0, groups, read_group, 0)

    for d in range(1, n):
        sq_copy(d, source(d)).wait_recv()
    total = sq[0]
    for p in range(1, n):
        total += sq[p]
    s_row = lax.rsqrt(total[:, 0:batch] / (n * width) + epsilon)
    s_col = to_col(s_row)
    for copy in (l_wi, l_wf, l_bi, l_bf, l_nrm, l_stab):
        copy.wait()
    w_both = jnp.concatenate([wi[...], wf[...]], axis=0)
    pre = jnp.zeros((2 * heads, batch), jnp.float32)
    for p in range(n):
        pre += dot(w_both[:, p * width : (p + 1) * width], xs[p], NT)
    pre = pre * s_row
    eye_h = lax.broadcasted_iota(jnp.int32, (heads, heads), 0) == lax.broadcasted_iota(jnp.int32, (heads, heads), 1)
    bias_i = jnp.sum(jnp.where(eye_h, bi[...], 0.0), axis=1, keepdims=True)
    bias_f = jnp.sum(jnp.where(eye_h, bf[...], 0.0), axis=1, keepdims=True)
    input_pre = pre[:heads] + bias_i
    forget_pre = pre[heads:] + bias_f
    log_forget = jnp.minimum(forget_pre, 0.0) - jnp.log1p(jnp.exp(-jnp.abs(forget_pre)))
    carried = log_forget + stab[...]
    stab_new = jnp.maximum(carried, input_pre)
    stab_out[...] = stab_new
    i_gate = jnp.exp(input_pre - stab_new)
    f_gate = jnp.exp(carried - stab_new)

    key = k_raw * (s_col * key_scale)
    query = q_raw * s_col
    for h in range(heads):
        n_rows[:, h * rows : (h + 1) * rows] = nrm[:, h, :]
    ones = mine.astype(jnp.float32)
    nq = dot(ones, n_rows[...] * query, NT, lax.Precision.HIGHEST)
    kq = dot(ones, key * query, NT, lax.Precision.HIGHEST)
    for h in range(heads):
        den_send[h, 0:1, 0:batch] = nq[h : h + 1]
        den_send[h, 1:2, 0:batch] = kq[h : h + 1]

    l_wv.wait()
    value = jnp.zeros((batch, width), jnp.float32)
    for p in range(n):
        value += dot(xs[p], wv[p * width : (p + 1) * width, :])
    value = (value * s_col).astype(jnp.bfloat16)
    vals[me] = value
    for d in range(1, n):
        den_copy(d).start()
    l_wg.wait()
    gate = jnp.zeros((batch, width), jnp.float32)
    for p in range(n):
        gate += dot(xs[p], wg[p * width : (p + 1) * width, :])
    gate = jax.nn.sigmoid(gate * s_col)
    for d in range(1, n):
        val_copy(d, me).start()

    key_t = jnp.transpose(key)
    for h in range(heads):
        at = slice(h * rows, (h + 1) * rows)
        ik = key_t[at, :] * i_gate[h : h + 1, :]
        fg = jnp.broadcast_to(f_gate[h : h + 1, :], (rows, batch))
        for g in range(groups):
            kcols[g, at, :] = ik[:, g * GROUP : (g + 1) * GROUP]
            fcols[g, at, :] = fg[:, g * GROUP : (g + 1) * GROUP]
    for h in range(heads):
        nrm_out[:, h, :] = to_col(f_gate[h : h + 1, :]) * nrm[:, h, :] + (
            to_col(i_gate[h : h + 1, :]) * key[:, h * rows : (h + 1) * rows]
        )

    my_head = lax.div(me * width, share)
    picked = lax.broadcasted_iota(jnp.int32, (heads, batch), 0) == my_head

    def pick(table):
        return jnp.sum(jnp.where(picked, table, 0.0), axis=0, keepdims=True)

    den = den_send[my_head]
    for d in range(1, n):
        den_copy(d).wait_recv()
        den += den_recv[d - 1]
    f_row, i_row, stab_row = pick(f_gate), pick(i_gate), pick(stab_new)
    nq_row, kq_row = den[0:1, 0:batch], den[1:2, 0:batch]
    denom = f_row * nq_row + i_row * kq_row
    bound = jnp.maximum(jnp.abs(denom), jnp.exp(-stab_row))
    mem_weight = to_col(f_row * s_row / bound)
    value_weight = to_col(i_row * kq_row / bound)
    l_wo.wait()
    numer = num_send[me].astype(jnp.float32)
    for d in range(1, n):
        for g in range(groups):
            num_copy(d, g).wait_recv()
        numer += num_recv[d - 1].astype(jnp.float32)
    numer = numer.reshape(batch, width)
    readout = mem_weight * numer + value_weight * value.astype(jnp.float32)
    hidden = (gate * readout).astype(jnp.bfloat16)

    def project(p):
        return dot(hidden, wo[:, pl.ds(pl.multiple_of(p * width, width), width)])

    for d in range(1, n):
        out_send[d - 1] = project(peer(d)).astype(jnp.bfloat16)
        if d > 1:
            out_copy(d - 1).start()
    branch = project(me)
    out_copy(n - 1).start()

    for p in range(n):
        if p:
            val_copy(p, source(p)).wait_recv()
    for p in range(n):
        val_rows[:, p * width : (p + 1) * width] = vals[p].astype(jnp.float32)

    def update_group(g, carry):
        for j in range(GROUP):
            b = g * GROUP + j
            for h in range(heads):
                at = slice(h * rows, (h + 1) * rows)
                fg = fcols[g, at, j : j + 1]
                ik = kcols[g, at, j : j + 1]
                val = val_rows[pl.ds(b, 1), h * dv : (h + 1) * dv]
                mem_out[b, at, :] = (fg * mem[b, at, :].astype(jnp.float32) + ik * val).astype(jnp.bfloat16)
        return carry

    lax.fori_loop(0, groups, update_group, 0)

    for d in range(1, n):
        out_copy(d).wait_recv()
        branch += out_recv[d - 1].astype(jnp.float32)
    res_out[...] = res[...] + branch

    for d in range(1, n):
        x_copy(d, me).wait_send()
        sq_copy(d, me).wait_send()
        val_copy(d, me).wait_send()
        den_copy(d).wait_send()
        out_copy(d).wait_send()
        for g in range(groups):
            num_copy(d, g).wait_send()


def write_back(res, mem, nrm, stab, res_out, mem_out, nrm_out, stab_out, sem):
    step = mem.shape[0] // PIECES
    pairs = [(mem.at[pl.ds(i * step, step)], mem_out.at[pl.ds(i * step, step)]) for i in range(PIECES)]
    pairs += [(res, res_out), (nrm, nrm_out), (stab, stab_out)]
    copies = [pltpu.make_async_copy(a, b, sem.at[i]) for i, (a, b) in enumerate(pairs)]
    for copy in copies:
        copy.start()
    for copy in copies:
        copy.wait()


def body(
    residual, norm_gain, w_query, w_key, w_value, w_gate, w_input, w_forget, b_input, b_forget, w_out, memory, normalizer, stabilizer
):
    n = lax.axis_size("head")
    batch, width = residual.shape
    heads, rows, d_model = w_query.shape
    dv = memory.shape[3]
    hr = heads * rows
    groups = batch // GROUP
    f32, bf16 = jnp.float32, jnp.bfloat16
    args = (
        residual,
        norm_gain.reshape(1, d_model),
        w_query.reshape(hr, d_model),
        w_key.reshape(hr, d_model),
        w_value,
        w_gate,
        w_input,
        w_forget,
        b_input.reshape(1, heads),
        b_forget.reshape(1, heads),
        w_out,
        memory.reshape(batch, hr, dv),
        normalizer,
        stabilizer.T,
    )
    args = tuple(pltpu.with_memory_space_constraint(a, pltpu.HBM) for a in args)
    local = [pltpu.VMEM(a.shape, a.dtype) for a in args]
    local[1] = pltpu.VMEM((1, width), f32)
    dma = pltpu.SemaphoreType.DMA
    scratch = local + [
        pltpu.VMEM((n, batch, width), bf16),
        pltpu.VMEM((n, 1, LANES), f32),
        pltpu.VMEM((n, groups, GROUP, width), bf16),
        pltpu.VMEM((n - 1, groups, GROUP, width), bf16),
        pltpu.VMEM((heads, 2, LANES), f32),
        pltpu.VMEM((n - 1, 2, LANES), f32),
        pltpu.VMEM((n, batch, width), bf16),
        pltpu.VMEM((n - 1, batch, width), bf16),
        pltpu.VMEM((n - 1, batch, width), bf16),
        pltpu.VMEM((batch, hr), f32),
        pltpu.VMEM((batch, hr), f32),
        pltpu.VMEM((heads, GROUP, dv), f32),
        pltpu.VMEM((batch, n * width), f32),
        pltpu.VMEM((groups, hr, GROUP), f32),
        pltpu.VMEM((groups, hr, GROUP), f32),
        dma((13,)),
        dma((groups,)),
        dma((n - 1,)), dma((n - 1,)),
        dma((n - 1,)), dma((n - 1,)),
        dma((n - 1, groups)), dma((n - 1, groups)),
        dma((n - 1,)), dma((n - 1,)),
        dma((n - 1,)), dma((n - 1,)),
        dma((n - 1,)), dma((n - 1,)),
    ]
    res_out, mem_out, nrm_out, stab_out = pl.pallas_call(
        functools.partial(kernel, n, batch, heads, rows, dv, width, 1.0 / math.sqrt(rows * n)),
        out_shape=(
            pltpu.VMEM((batch, width), f32),
            pltpu.VMEM((batch, hr, dv), bf16),
            pltpu.VMEM(normalizer.shape, f32),
            pltpu.VMEM((heads, batch), f32),
        ),
        in_specs=[pl.BlockSpec(memory_space=pltpu.HBM)] * len(args),
        out_specs=(pl.BlockSpec(memory_space=pltpu.VMEM),) * 4,
        scratch_shapes=scratch,
        compiler_params=pltpu.CompilerParams(collective_id=0, has_side_effects=True, vmem_limit_bytes=40 * 1024 * 1024),
        name="mlstm_step",
    )(*args)
    results = (res_out, mem_out, nrm_out, stab_out)
    res_out, mem_out, nrm_out, stab_out = pl.pallas_call(
        write_back,
        out_shape=tuple(jax.ShapeDtypeStruct(a.shape, a.dtype) for a in results),
        in_specs=[pl.BlockSpec(memory_space=pltpu.VMEM)] * 4,
        out_specs=(pl.BlockSpec(memory_space=pltpu.HBM),) * 4,
        scratch_shapes=[dma((3 + PIECES,))],
        compiler_params=pltpu.CompilerParams(vmem_limit_bytes=1024 * 1024),
        name="write_back",
    )(*(pltpu.with_memory_space_constraint(a, pltpu.VMEM) for a in results))
    return res_out, mem_out.reshape(memory.shape), nrm_out, stab_out.T


def solution(mesh):
    in_specs = (
        P("dp", "head"),
        P(),
        P(None, "head", None),
        P(None, "head", None),
        P(None, "head"),
        P(None, "head"),
        P(),
        P(),
        P(),
        P(),
        P("head", None),
        P("dp", None, "head", None),
        P("dp", None, "head"),
        P("dp", None),
    )
    out_specs = (P("dp", "head"), P("dp", None, "head", None), P("dp", None, "head"), P("dp", None))
    return jax.shard_map(body, mesh=mesh, in_specs=in_specs, out_specs=out_specs, check_vma=False)
```

profile of v0, /device:TPU:0, one launch (start us, length us, event | category | flops | bytes accessed | tf_op | source)
XLA Modules:
  0.0 23.1 jit_solution(10355165519328334066)
XLA Ops:
  0.6 19.7 %mlstm_step.1 = (f32[24,512]{1,0:T(8,128)S(1)}, bf16[24,256,512]{2,1,0:T(8,128)(2,1)S(1)}, f32[24,8,32]{2,1,0:T(8,128)S(1)}, f32[8,24]{1,0:T(8,128)S(1)}) custom-call(f32[24,512]{1,0:T(8,128)} %res_hbm.1, f32[1,4096]{1,0:T(1,128)} %bitcast.12, bf16[256,4096]{1,0:T(8,128)(2,1)} %bitcast.10, bf16[256,4096]{1,0:T(8,128)(2,1)} %bitcast.11, ...), custom_call_target="tpu_custom_call" | custom-call | tf_op jit(solution)/shard_map/mlstm_step/pallas_call | solution.py:351
  20.4 2.8 %write_back.1 = (f32[24,512]{1,0:T(8,128)}, bf16[24,256,512]{2,1,0:T(8,128)(2,1)}, f32[24,8,32]{2,1,0:T(8,128)}, f32[8,24]{1,0:T(8,128)}) custom-call(f32[24,512]{1,0:T(8,128)S(1)} %get-tuple-element.12.res, bf16[24,256,512]{2,1,0:T(8,128)(2,1)S(1)} %get-tuple-element.13.mem, f32[24,8,32]{2,1,0:T(8,128)S(1)} %get-tuple-element.14.nrm, ...), custom_call_target="tpu_custom_call" | custom-call | tf_op jit(solution)/shard_map/write_back/pallas_call | solution.py:366
where the time goes:
time: 23.3 us; the launch traced here: 23.1 us
  Pallas kernels  22.5 us (97%)
  between operations  0.64 us (3%)
    pallas_call x1, Pallas kernels, body(): pl.pallas_call(functools.partial(kernel, n, batch, heads, rows, dv, width...  19.7 us
    pallas_call x1, Pallas kernels, body(): pl.pallas_call(write_back, out_shape=tuple((jax.ShapeDtypeStruct(a.shape,...  2.77 us

commit v1 on v0

--- a/solution.py
+++ b/solution.py
@@ -27,7 +27,7 @@
     res_out, mem_out, nrm_out, stab_out,
     res, gain, wq, wk, wv, wg, wi, wf, bi, bf, wo, mem, nrm, stab,
     xs, sq, num_send, num_recv, den_send, den_recv, vals, out_send, out_recv,
-    q_rows, n_rows, num_tile, val_rows, fcols, kcols,
+    kt_ref, n_rows, num_tile, val_rows, f_rows, kcols,
     in_sem, mem_sem, x_send, x_recv, sq_send, sq_recv, num_ss, num_rs, den_ss, den_rs, val_ss, val_rs, out_ss, out_rs,
 ):
     me = lax.axis_index("head")
@@ -37,12 +37,20 @@
     barrier = pltpu.get_barrier_semaphore()
 
     def peer(d):
-        return lax.rem(me + d, n)
-
-    def source(d):
-        return lax.rem(me + n - d, n)
-
-    for d in range(1, n):
+        other = me
+        for k in range(n.bit_length() - 1):
+            if d >> k & 1:
+                other += (1 << k) * (1 - 2 * lax.rem(lax.div(me, 1 << k), 2))
+        return other
+
+    source = peer
+
+    def other(k):
+        return k + lax.div(k + n - me, n)
+
+    far_first = sorted(range(1, n), key=lambda d: (-(d >> 1).bit_count(), d % 2))
+
+    for d in far_first:
         pl.semaphore_signal(barrier, inc=1, device_id={"head": peer(d)}, device_id_type=pl.DeviceIdType.MESH)
 
     gain_part = gain_hbm.at[:, pl.ds(pl.multiple_of(me * width, width), width)]
@@ -103,34 +111,36 @@
         head = lax.div(peer(d) * width, share)
         return remote(den_send.at[head], den_recv.at[d - 1], den_ss.at[d - 1], den_rs.at[d - 1], peer(d))
 
-    def out_copy(d):
-        return remote(out_send.at[d - 1], out_recv.at[d - 1], out_ss.at[d - 1], out_rs.at[d - 1], peer(d))
+    def out_copy(k, owner, target):
+        return remote(out_send.at[k], out_recv.at[owner], out_ss.at[k], out_rs.at[owner], target)
 
     pl.semaphore_wait(barrier, n - 1)
-    for d in range(1, n):
+    for d in [1, 3, 5, 7, 2, 4, 6]:
         x_copy(d, me).start()
-    for d in range(1, n):
+    for d in far_first:
         sq_copy(d, me).start()
 
     l_wq.wait()
     l_wk.wait()
-    q_raw = jnp.zeros((batch, hr), jnp.float32)
-    k_raw = jnp.zeros((batch, hr), jnp.float32)
-    for d in range(n):
+    l_nrm.wait()
+    q_t = jnp.zeros((hr, batch), jnp.float32)
+    k_t = jnp.zeros((hr, batch), jnp.float32)
+    for d in [0, 1, 3, 5, 2, 4, 7, 6]:
         owner = source(d)
         if d:
-            x_copy(d, owner).wait_recv()
+            with jax.named_scope(f"qk{d}_wait"):
+                x_copy(d, owner).wait_recv()
         cols = pl.ds(pl.multiple_of(owner * width, width), width)
         block = xs[owner]
-        q_raw += dot(block, wq[:, cols], NT)
-        k_raw += dot(block, wk[:, cols], NT)
-    q_rows[...] = q_raw
+        q_t += dot(wq[:, cols], block, NT)
+        k_t += dot(wk[:, cols], block, NT)
+    kt_ref[...] = k_t
+    q_raw = jnp.transpose(q_t)
 
     mine = lax.broadcasted_iota(jnp.int32, (heads, hr), 1) // rows == lax.broadcasted_iota(jnp.int32, (heads, hr), 0)
 
-    def read_group(g, carry):
-        mem_load(g).wait()
-        block_q = q_rows[pl.ds(pl.multiple_of(g * GROUP, GROUP), GROUP), :]
+    def numerators(g):
+        block_q = q_raw[g * GROUP : (g + 1) * GROUP, :]
         for j in range(GROUP):
             spread = jnp.where(mine, block_q[j : j + 1, :], 0.0)
             high = spread.astype(jnp.bfloat16)
@@ -140,20 +150,46 @@
         for p in range(n):
             head, col = p * width // dv, p * width % dv
             num_send[p, g] = num_tile[head, :, col : col + width].astype(jnp.bfloat16)
-        for d in range(1, n):
+
+    def split_sum(product):
+        high = product.astype(jnp.bfloat16)
+        low = (product - high.astype(jnp.float32)).astype(jnp.bfloat16)
+        return dot(ones, high, NT) + dot(ones, low, NT)
+
+    ones = mine.astype(jnp.bfloat16)
+    for g in range(groups):
+        mem_load(g).wait()
+        numerators(g)
+        if g == groups - 1:
+            k_raw = jnp.transpose(kt_ref[...])
+            for h in range(heads):
+                n_rows[:, h * rows : (h + 1) * rows] = nrm[:, h, :]
+            nq = split_sum(n_rows[...] * q_raw)
+            kq = split_sum(k_raw * q_raw)
+            for h in range(heads):
+                den_send[h, 0:1, 0:batch] = nq[h : h + 1]
+                den_send[h, 1:2, 0:batch] = kq[h : h + 1]
+        for d in far_first:
             num_copy(d, g).start()
-        return carry
-
-    lax.fori_loop(0, groups, read_group, 0)
-
-    for d in range(1, n):
+    for d in far_first:
+        den_copy(d).start()
+    for d in far_first:
         sq_copy(d, source(d)).wait_recv()
     total = sq[0]
     for p in range(1, n):
         total += sq[p]
     s_row = lax.rsqrt(total[:, 0:batch] / (n * width) + epsilon)
     s_col = to_col(s_row)
-    for copy in (l_wi, l_wf, l_bi, l_bf, l_nrm, l_stab):
+    l_wv.wait()
+    value = jnp.zeros((batch, width), jnp.float32)
+    for p in range(n):
+        value += dot(xs[p], wv[p * width : (p + 1) * width, :])
+    value = (value * s_col).astype(jnp.bfloat16)
+    vals[me] = value
+    for d in far_first:
+        val_copy(d, me).start()
+
+    for copy in (l_wi, l_wf, l_bi, l_bf, l_stab):
         copy.wait()
     w_both = jnp.concatenate([wi[...], wf[...]], axis=0)
     pre = jnp.zeros((2 * heads, batch), jnp.float32)
@@ -173,40 +209,23 @@
     f_gate = jnp.exp(carried - stab_new)
 
     key = k_raw * (s_col * key_scale)
-    query = q_raw * s_col
-    for h in range(heads):
-        n_rows[:, h * rows : (h + 1) * rows] = nrm[:, h, :]
-    ones = mine.astype(jnp.float32)
-    nq = dot(ones, n_rows[...] * query, NT, lax.Precision.HIGHEST)
-    kq = dot(ones, key * query, NT, lax.Precision.HIGHEST)
-    for h in range(heads):
-        den_send[h, 0:1, 0:batch] = nq[h : h + 1]
-        den_send[h, 1:2, 0:batch] = kq[h : h + 1]
-
-    l_wv.wait()
-    value = jnp.zeros((batch, width), jnp.float32)
+    l_wg.wait()
+    cuts = 2 if width % (2 * LANES) == 0 else 1
+    half = width // cuts
+    gates2 = [jnp.zeros((batch, half), jnp.float32) for _ in range(cuts)]
     for p in range(n):
-        value += dot(xs[p], wv[p * width : (p + 1) * width, :])
-    value = (value * s_col).astype(jnp.bfloat16)
-    vals[me] = value
-    for d in range(1, n):
-        den_copy(d).start()
-    l_wg.wait()
-    gate = jnp.zeros((batch, width), jnp.float32)
-    for p in range(n):
-        gate += dot(xs[p], wg[p * width : (p + 1) * width, :])
+        for e in range(cuts):
+            gates2[e] += dot(xs[p], wg[p * width : (p + 1) * width, e * half : (e + 1) * half])
+    gate = jnp.concatenate(gates2, axis=1)
     gate = jax.nn.sigmoid(gate * s_col)
-    for d in range(1, n):
-        val_copy(d, me).start()
-
-    key_t = jnp.transpose(key)
+
+    key_t = kt_ref[...] * (s_row * key_scale)
     for h in range(heads):
         at = slice(h * rows, (h + 1) * rows)
         ik = key_t[at, :] * i_gate[h : h + 1, :]
-        fg = jnp.broadcast_to(f_gate[h : h + 1, :], (rows, batch))
+        f_rows[h] = jnp.broadcast_to(to_col(f_gate[h : h + 1, :]), (batch, LANES)).reshape(groups, GROUP, LANES)
         for g in range(groups):
             kcols[g, at, :] = ik[:, g * GROUP : (g + 1) * GROUP]
-            fcols[g, at, :] = fg[:, g * GROUP : (g + 1) * GROUP]
     for h in range(heads):
         nrm_out[:, h, :] = to_col(f_gate[h : h + 1, :]) * nrm[:, h, :] + (
             to_col(i_gate[h : h + 1, :]) * key[:, h * rows : (h + 1) * rows]
@@ -223,7 +242,8 @@
         den_copy(d).wait_recv()
         den += den_recv[d - 1]
     f_row, i_row, stab_row = pick(f_gate), pick(i_gate), pick(stab_new)
-    nq_row, kq_row = den[0:1, 0:batch], den[1:2, 0:batch]
+    nq_row = den[0:1, 0:batch] * s_row
+    kq_row = den[1:2, 0:batch] * (s_row * s_row * key_scale)
     denom = f_row * nq_row + i_row * kq_row
     bound = jnp.maximum(jnp.abs(denom), jnp.exp(-stab_row))
     mem_weight = to_col(f_row * s_row / bound)
@@ -239,37 +259,37 @@
     hidden = (gate * readout).astype(jnp.bfloat16)
 
     def project(p):
-        return dot(hidden, wo[:, pl.ds(pl.multiple_of(p * width, width), width)])
-
-    for d in range(1, n):
-        out_send[d - 1] = project(peer(d)).astype(jnp.bfloat16)
-        if d > 1:
-            out_copy(d - 1).start()
+        return jnp.concatenate(
+            [dot(hidden, wo[:, pl.ds(pl.multiple_of(p * width + e * half, half), half)]) for e in range(cuts)], axis=1
+        )
+
+    for k in range(n - 1):
+        out_send[k] = project(other(k)).astype(jnp.bfloat16)
+        out_copy(k, me, other(k)).start()
     branch = project(me)
-    out_copy(n - 1).start()
-
+    for d in far_first:
+        val_copy(d, source(d)).wait_recv()
     for p in range(n):
-        if p:
-            val_copy(p, source(p)).wait_recv()
-    for p in range(n):
-        val_rows[:, p * width : (p + 1) * width] = vals[p].astype(jnp.float32)
+        val_rows[:, :, p * width : (p + 1) * width] = vals[p].astype(jnp.float32).reshape(groups, GROUP, width)
 
     def update_group(g, carry):
         for j in range(GROUP):
             b = g * GROUP + j
             for h in range(heads):
                 at = slice(h * rows, (h + 1) * rows)
-                fg = fcols[g, at, j : j + 1]
-                ik = kcols[g, at, j : j + 1]
-                val = val_rows[pl.ds(b, 1), h * dv : (h + 1) * dv]
-                mem_out[b, at, :] = (fg * mem[b, at, :].astype(jnp.float32) + ik * val).astype(jnp.bfloat16)
+                fg = jnp.broadcast_to(f_rows[h, g, j : j + 1, :], (rows, LANES)).astype(jnp.bfloat16)
+                ik = jnp.broadcast_to(kcols[g, at, j : j + 1], (rows, LANES)).astype(jnp.bfloat16)
+                for c in range(0, dv, LANES):
+                    val = val_rows[g, j : j + 1, h * dv + c : h * dv + c + LANES]
+                    val = jnp.broadcast_to(val, (rows, LANES)).astype(jnp.bfloat16)
+                    mem_out[b, at, c : c + LANES] = fg * mem[b, at, c : c + LANES] + ik * val
         return carry
 
     lax.fori_loop(0, groups, update_group, 0)
-
     for d in range(1, n):
-        out_copy(d).wait_recv()
-        branch += out_recv[d - 1].astype(jnp.float32)
+        owner = source(d)
+        out_copy(0, owner, owner).wait_recv()
+        branch += out_recv[owner].astype(jnp.float32)
     res_out[...] = res[...] + branch
 
     for d in range(1, n):
@@ -277,7 +297,7 @@
         sq_copy(d, me).wait_send()
         val_copy(d, me).wait_send()
         den_copy(d).wait_send()
-        out_copy(d).wait_send()
+        out_copy(d - 1, me, me).wait_send()
         for g in range(groups):
             num_copy(d, g).wait_send()
 
@@ -332,12 +352,12 @@
         pltpu.VMEM((n - 1, 2, LANES), f32),
         pltpu.VMEM((n, batch, width), bf16),
         pltpu.VMEM((n - 1, batch, width), bf16),
-        pltpu.VMEM((n - 1, batch, width), bf16),
-        pltpu.VMEM((batch, hr), f32),
+        pltpu.VMEM((n, batch, width), bf16),
+        pltpu.VMEM((hr, batch), f32),
         pltpu.VMEM((batch, hr), f32),
         pltpu.VMEM((heads, GROUP, dv), f32),
-        pltpu.VMEM((batch, n * width), f32),
-        pltpu.VMEM((groups, hr, GROUP), f32),
+        pltpu.VMEM((groups, GROUP, n * width), f32),
+        pltpu.VMEM((heads, groups, GROUP, LANES), f32),
         pltpu.VMEM((groups, hr, GROUP), f32),
         dma((13,)),
         dma((groups,)),
@@ -346,7 +366,7 @@
         dma((n - 1, groups)), dma((n - 1, groups)),
         dma((n - 1,)), dma((n - 1,)),
         dma((n - 1,)), dma((n - 1,)),
-        dma((n - 1,)), dma((n - 1,)),
+        dma((n - 1,)), dma((n,)),
     ]
     res_out, mem_out, nrm_out, stab_out = pl.pallas_call(
         functools.partial(kernel, n, batch, heads, rows, dv, width, 1.0 / math.sqrt(rows * n)),

time: 23.3 us -> 22.7 us (0.974)
  Pallas kernels: 22.5 us -> 21.9 us
    pallas_call x1, Pallas kernels: 19.7 us -> 19.2 us  [body(): pl.pallas_call(functools.partial(kernel, n, batch, heads, rows, dv, width...]
where the time goes in v1:
time: 22.7 us; the launch traced here: 22.6 us
  Pallas kernels  21.9 us (96%)
  between operations  0.64 us (3%)
    pallas_call x1, Pallas kernels, body(): pl.pallas_call(functools.partial(kernel, n, batch, heads, rows, dv, width...  19.2 us
    pallas_call x1, Pallas kernels, body(): pl.pallas_call(write_back, out_shape=tuple((jax.ShapeDtypeStruct(a.shape,...  2.77 us

profile of v1, /device:TPU:0, one launch (start us, length us, event | category | flops | bytes accessed | tf_op | source)
XLA Modules:
  0.0 22.6 jit_solution(17745326103391540955)
XLA Ops:
  0.6 19.2 %mlstm_step.1 = (f32[24,512]{1,0:T(8,128)S(1)}, bf16[24,256,512]{2,1,0:T(8,128)(2,1)S(1)}, f32[24,8,32]{2,1,0:T(8,128)S(1)}, f32[8,24]{1,0:T(8,128)S(1)}) custom-call(f32[24,512]{1,0:T(8,128)} %res_hbm.1, f32[1,4096]{1,0:T(1,128)} %bitcast.12, bf16[256,4096]{1,0:T(8,128)(2,1)} %bitcast.10, bf16[256,4096]{1,0:T(8,128)(2,1)} %bitcast.11, ...), custom_call_target="tpu_custom_call" | custom-call | tf_op jit(solution)/shard_map/mlstm_step/pallas_call | solution.py:371
  19.8 2.8 %write_back.1 = (f32[24,512]{1,0:T(8,128)}, bf16[24,256,512]{2,1,0:T(8,128)(2,1)}, f32[24,8,32]{2,1,0:T(8,128)}, f32[8,24]{1,0:T(8,128)}) custom-call(f32[24,512]{1,0:T(8,128)S(1)} %get-tuple-element.12.res, bf16[24,256,512]{2,1,0:T(8,128)(2,1)S(1)} %get-tuple-element.13.mem, f32[24,8,32]{2,1,0:T(8,128)S(1)} %get-tuple-element.14.nrm, ...), custom_call_target="tpu_custom_call" | custom-call | tf_op jit(solution)/shard_map/write_back/pallas_call | solution.py:386

commit v2 on v1

--- a/solution.py
+++ b/solution.py
@@ -10,7 +10,9 @@
 
 GROUP = 8
 LANES = 128
-PIECES = 4
+STEP = 8
+EARLY = 2
+SUMMED = 2
 epsilon = 1e-06
 
 NT = (((1,), (1,)), ((), ()))
@@ -19,15 +21,43 @@
 
 def dot(a, b, dims=NN, precision=None):
     return lax.dot_general(a, b, dims, precision=precision, preferred_element_type=jnp.float32)
+
+
+def spread_values(vals, val_rows):
+    n, batch, width = vals.shape
+    for p in range(n):
+        val_rows[p] = vals[p].astype(jnp.float32).reshape(batch // GROUP, GROUP, width)
+
+
+def update_group(mem, mem_out, val_rows, f_rows, kcols, g):
+    n, width = val_rows.shape[0], val_rows.shape[3]
+    rows, dv = mem.shape[1] // f_rows.shape[0], mem.shape[2]
+
+    def step(i, carry):
+        for t in range(STEP):
+            j = t
+            b = g * GROUP + i * STEP + t
+            for p in range(n):
+                h, base = p * width // dv, p * width % dv
+                at = slice(h * rows, (h + 1) * rows)
+                fg = jnp.broadcast_to(f_rows[h, g, j : j + 1, :], (rows, LANES)).astype(jnp.bfloat16)
+                ik = jnp.broadcast_to(kcols[g, at, j : j + 1], (rows, LANES)).astype(jnp.bfloat16)
+                for c in range(0, width, LANES):
+                    val = jnp.broadcast_to(val_rows[p, g, j : j + 1, c : c + LANES], (rows, LANES)).astype(jnp.bfloat16)
+                    cols = slice(base + c, base + c + LANES)
+                    mem_out[b, at, cols] = fg * mem[b, at, cols] + ik * val
+        return carry
+
+    lax.fori_loop(0, GROUP // STEP, step, 0)
 
 
 def kernel(
     n, batch, heads, rows, dv, width, key_scale,
     res_hbm, gain_hbm, wq_hbm, wk_hbm, wv_hbm, wg_hbm, wi_hbm, wf_hbm, bi_hbm, bf_hbm, wo_hbm, mem_hbm, nrm_hbm, stab_hbm,
-    res_out, mem_out, nrm_out, stab_out,
-    res, gain, wq, wk, wv, wg, wi, wf, bi, bf, wo, mem, nrm, stab,
-    xs, sq, num_send, num_recv, den_send, den_recv, vals, out_send, out_recv,
-    kt_ref, n_rows, num_tile, val_rows, f_rows, kcols,
+    res_out, mem, nrm_out, stab_out, vals, kcols, f_rows,
+    res, gain, wq, wk, wv, wg, wi, wf, bi, bf, wo, nrm, stab,
+    xs, sq, num_send, num_recv, den_send, den_recv, out_send, out_recv,
+    kt_ref, qt_ref, n_rows, num_tile, val_rows,
     in_sem, mem_sem, x_send, x_recv, sq_send, sq_recv, num_ss, num_rs, den_ss, den_rs, val_ss, val_rs, out_ss, out_rs,
 ):
     me = lax.axis_index("head")
@@ -50,6 +80,9 @@
 
     far_first = sorted(range(1, n), key=lambda d: (-(d >> 1).bit_count(), d % 2))
 
+    near = [d for d in far_first if d % 2 == 0] + [1]
+    far = [d for d in far_first if d % 2 and d > 1]
+
     for d in far_first:
         pl.semaphore_signal(barrier, inc=1, device_id={"head": peer(d)}, device_id_type=pl.DeviceIdType.MESH)
 
@@ -96,23 +129,30 @@
     den_send[...] = jnp.zeros_like(den_send)
 
     def x_copy(d, owner):
-        return remote(xs.at[owner], xs.at[owner], x_send.at[d - 1], x_recv.at[d - 1], peer(d))
+        return remote(xs.at[owner], xs.at[owner], x_send, x_recv.at[d - 1], peer(d))
 
     def sq_copy(d, owner):
-        return remote(sq.at[owner], sq.at[owner], sq_send.at[d - 1], sq_recv.at[d - 1], peer(d))
+        return remote(sq.at[owner], sq.at[owner], sq_send, sq_recv, peer(d))
 
     def val_copy(d, owner):
-        return remote(vals.at[owner], vals.at[owner], val_ss.at[d - 1], val_rs.at[d - 1], peer(d))
+        return remote(vals.at[owner], vals.at[owner], val_ss, val_rs.at[0 if d == 1 else 1 + d % 2], peer(d))
+
+    def val_relay(d):
+        return remote(vals.at[peer(d)], vals.at[peer(d)], val_ss, val_rs.at[2], peer(1))
 
     def num_copy(d, g):
-        return remote(num_send.at[peer(d), g], num_recv.at[d - 1, g], num_ss.at[d - 1, g], num_rs.at[d - 1, g], peer(d))
+        return remote(num_send.at[peer(d), g], num_recv.at[d - 1, g], num_ss, num_rs, peer(d))
 
     def den_copy(d):
         head = lax.div(peer(d) * width, share)
-        return remote(den_send.at[head], den_recv.at[d - 1], den_ss.at[d - 1], den_rs.at[d - 1], peer(d))
-
-    def out_copy(k, owner, target):
-        return remote(out_send.at[k], out_recv.at[owner], out_ss.at[k], out_rs.at[owner], target)
+        return remote(den_send.at[head], den_recv.at[d - 1], den_ss, den_rs, peer(d))
+
+    def out_copy(k):
+        target = other(k)
+        return remote(out_send.at[k], out_recv.at[lax.rem(me + n - target, n) - 1], out_ss, out_rs, target)
+
+    def whole(ref, ssem, rsem):
+        return remote(ref, ref, ssem, rsem, peer(1))
 
     pl.semaphore_wait(barrier, n - 1)
     for d in [1, 3, 5, 7, 2, 4, 6]:
@@ -135,18 +175,27 @@
         q_t += dot(wq[:, cols], block, NT)
         k_t += dot(wk[:, cols], block, NT)
     kt_ref[...] = k_t
+    qt_ref[...] = q_t
     q_raw = jnp.transpose(q_t)
 
     mine = lax.broadcasted_iota(jnp.int32, (heads, hr), 1) // rows == lax.broadcasted_iota(jnp.int32, (heads, hr), 0)
 
     def numerators(g):
         block_q = q_raw[g * GROUP : (g + 1) * GROUP, :]
-        for j in range(GROUP):
+        for j in range(SUMMED, GROUP):
             spread = jnp.where(mine, block_q[j : j + 1, :], 0.0)
             high = spread.astype(jnp.bfloat16)
             low = (spread - high.astype(jnp.float32)).astype(jnp.bfloat16)
             both = dot(jnp.concatenate([high, low], axis=0), mem[g * GROUP + j])
             num_tile[:, j, :] = both[:heads] + both[heads:]
+        for j in range(SUMMED):
+            b = g * GROUP + j
+            for h in range(heads):
+                at = slice(h * rows, (h + 1) * rows)
+                weight = jnp.broadcast_to(qt_ref[at, b : b + 1], (rows, LANES))
+                for c in range(0, dv, LANES):
+                    product = mem[b, at, c : c + LANES].astype(jnp.float32) * weight
+                    num_tile[h, j : j + 1, c : c + LANES] = jnp.sum(product, axis=0, keepdims=True)
         for p in range(n):
             head, col = p * width // dv, p * width % dv
             num_send[p, g] = num_tile[head, :, col : col + width].astype(jnp.bfloat16)
@@ -173,8 +222,8 @@
             num_copy(d, g).start()
     for d in far_first:
         den_copy(d).start()
-    for d in far_first:
-        sq_copy(d, source(d)).wait_recv()
+    all_sq = whole(sq.at[pl.ds(0, n - 1)], sq_send, sq_recv)
+    all_sq.wait_recv()
     total = sq[0]
     for p in range(1, n):
         total += sq[p]
@@ -186,8 +235,6 @@
         value += dot(xs[p], wv[p * width : (p + 1) * width, :])
     value = (value * s_col).astype(jnp.bfloat16)
     vals[me] = value
-    for d in far_first:
-        val_copy(d, me).start()
 
     for copy in (l_wi, l_wf, l_bi, l_bf, l_stab):
         copy.wait()
@@ -218,6 +265,8 @@
             gates2[e] += dot(xs[p], wg[p * width : (p + 1) * width, e * half : (e + 1) * half])
     gate = jnp.concatenate(gates2, axis=1)
     gate = jax.nn.sigmoid(gate * s_col)
+    for d in near:
+        val_copy(d, me).start()
 
     key_t = kt_ref[...] * (s_row * key_scale)
     for h in range(heads):
@@ -238,8 +287,9 @@
         return jnp.sum(jnp.where(picked, table, 0.0), axis=0, keepdims=True)
 
     den = den_send[my_head]
+    all_den = whole(den_recv, den_ss, den_rs)
+    all_den.wait_recv()
     for d in range(1, n):
-        den_copy(d).wait_recv()
         den += den_recv[d - 1]
     f_row, i_row, stab_row = pick(f_gate), pick(i_gate), pick(stab_new)
     nq_row = den[0:1, 0:batch] * s_row
@@ -250,9 +300,9 @@
     value_weight = to_col(i_row * kq_row / bound)
     l_wo.wait()
     numer = num_send[me].astype(jnp.float32)
+    all_num = whole(num_recv, num_ss, num_rs)
+    all_num.wait_recv()
     for d in range(1, n):
-        for g in range(groups):
-            num_copy(d, g).wait_recv()
         numer += num_recv[d - 1].astype(jnp.float32)
     numer = numer.reshape(batch, width)
     readout = mem_weight * numer + value_weight * value.astype(jnp.float32)
@@ -263,52 +313,55 @@
             [dot(hidden, wo[:, pl.ds(pl.multiple_of(p * width + e * half, half), half)]) for e in range(cuts)], axis=1
         )
 
-    for k in range(n - 1):
-        out_send[k] = project(other(k)).astype(jnp.bfloat16)
-        out_copy(k, me, other(k)).start()
-    branch = project(me)
-    for d in far_first:
-        val_copy(d, source(d)).wait_recv()
-    for p in range(n):
-        val_rows[:, :, p * width : (p + 1) * width] = vals[p].astype(jnp.float32).reshape(groups, GROUP, width)
-
-    def update_group(g, carry):
-        for j in range(GROUP):
-            b = g * GROUP + j
-            for h in range(heads):
-                at = slice(h * rows, (h + 1) * rows)
-                fg = jnp.broadcast_to(f_rows[h, g, j : j + 1, :], (rows, LANES)).astype(jnp.bfloat16)
-                ik = jnp.broadcast_to(kcols[g, at, j : j + 1], (rows, LANES)).astype(jnp.bfloat16)
-                for c in range(0, dv, LANES):
-                    val = val_rows[g, j : j + 1, h * dv + c : h * dv + c + LANES]
-                    val = jnp.broadcast_to(val, (rows, LANES)).astype(jnp.bfloat16)
-                    mem_out[b, at, c : c + LANES] = fg * mem[b, at, c : c + LANES] + ik * val
-        return carry
-
-    lax.fori_loop(0, groups, update_group, 0)
+    out_send[0] = project(other(0)).astype(jnp.bfloat16)
+    out_copy(0).start()
+    for k in range(1, n, 2):
+        for c in range(k, min(k + 2, n - 1)):
+            out_send[c] = project(other(c)).astype(jnp.bfloat16)
+        if k + 1 >= n - 1:
+            branch = project(me)
+        for c in range(k, min(k + 2, n - 1)):
+            out_copy(c).start()
+    if n > 2:
+        whole(vals.at[pl.ds(0, n // 2 - 1)], val_ss, val_rs.at[1]).wait_recv()
+    for d in near[:-1]:
+        val_relay(d).start()
+    val_copy(1, source(1)).wait_recv()
+    if n > 2:
+        whole(vals.at[pl.ds(0, n // 2 - 1)], val_ss, val_rs.at[2]).wait_recv()
+    spread_values(vals, val_rows)
+    for g in range(EARLY):
+        update_group(mem, mem, val_rows, f_rows, kcols, g)
+    all_out = whole(out_recv, out_ss, out_rs)
+    all_out.wait_recv()
     for d in range(1, n):
-        owner = source(d)
-        out_copy(0, owner, owner).wait_recv()
-        branch += out_recv[owner].astype(jnp.float32)
+        branch += out_recv[d - 1].astype(jnp.float32)
     res_out[...] = res[...] + branch
 
-    for d in range(1, n):
-        x_copy(d, me).wait_send()
-        sq_copy(d, me).wait_send()
-        val_copy(d, me).wait_send()
-        den_copy(d).wait_send()
-        out_copy(d - 1, me, me).wait_send()
-        for g in range(groups):
-            num_copy(d, g).wait_send()
-
-
-def write_back(res, mem, nrm, stab, res_out, mem_out, nrm_out, stab_out, sem):
-    step = mem.shape[0] // PIECES
-    pairs = [(mem.at[pl.ds(i * step, step)], mem_out.at[pl.ds(i * step, step)]) for i in range(PIECES)]
-    pairs += [(res, res_out), (nrm, nrm_out), (stab, stab_out)]
-    copies = [pltpu.make_async_copy(a, b, sem.at[i]) for i, (a, b) in enumerate(pairs)]
+    whole(xs.at[pl.ds(0, n - 1)], x_send, x_recv.at[0]).wait_send()
+    whole(vals.at[pl.ds(0, n - 1)], val_ss, val_rs.at[0]).wait_send()
+    for copy in (all_sq, all_num, all_den, all_out):
+        copy.wait_send()
+
+def write_back(res, mem, nrm, stab, vals, kcols, f_rows, res_out, mem_out, nrm_out, stab_out, staged, val_rows, sem):
+    groups = mem.shape[0] // GROUP
+
+    def block(g, source):
+        part = pl.ds(g * GROUP, GROUP)
+        return pltpu.make_async_copy(source.at[part], mem_out.at[part], sem.at[g])
+
+    copies = [block(g, mem) for g in range(EARLY)]
+    copies += [
+        pltpu.make_async_copy(a, b, sem.at[groups + i])
+        for i, (a, b) in enumerate([(res, res_out), (nrm, nrm_out), (stab, stab_out)])
+    ]
     for copy in copies:
         copy.start()
+    spread_values(vals, val_rows)
+    for g in range(EARLY, groups):
+        update_group(mem, staged, val_rows, f_rows, kcols, g)
+        copies.append(block(g, staged))
+        copies[-1].start()
     for copy in copies:
         copy.wait()
 
@@ -342,6 +395,7 @@
     args = tuple(pltpu.with_memory_space_constraint(a, pltpu.HBM) for a in args)
     local = [pltpu.VMEM(a.shape, a.dtype) for a in args]
     local[1] = pltpu.VMEM((1, width), f32)
+    del local[11]
     dma = pltpu.SemaphoreType.DMA
     scratch = local + [
         pltpu.VMEM((n, batch, width), bf16),
@@ -350,46 +404,48 @@
         pltpu.VMEM((n - 1, groups, GROUP, width), bf16),
         pltpu.VMEM((heads, 2, LANES), f32),
         pltpu.VMEM((n - 1, 2, LANES), f32),
-        pltpu.VMEM((n, batch, width), bf16),
         pltpu.VMEM((n - 1, batch, width), bf16),
-        pltpu.VMEM((n, batch, width), bf16),
+        pltpu.VMEM((n - 1, batch, width), bf16),
+        pltpu.VMEM((hr, batch), f32),
         pltpu.VMEM((hr, batch), f32),
         pltpu.VMEM((batch, hr), f32),
         pltpu.VMEM((heads, GROUP, dv), f32),
-        pltpu.VMEM((groups, GROUP, n * width), f32),
-        pltpu.VMEM((heads, groups, GROUP, LANES), f32),
-        pltpu.VMEM((groups, hr, GROUP), f32),
+        pltpu.VMEM((n, groups, GROUP, width), f32),
         dma((13,)),
         dma((groups,)),
-        dma((n - 1,)), dma((n - 1,)),
-        dma((n - 1,)), dma((n - 1,)),
-        dma((n - 1, groups)), dma((n - 1, groups)),
-        dma((n - 1,)), dma((n - 1,)),
-        dma((n - 1,)), dma((n - 1,)),
-        dma((n - 1,)), dma((n,)),
+        dma, dma((n - 1,)),
+        dma, dma, dma, dma, dma, dma,
+        dma, dma((3,)),
+        dma, dma,
     ]
-    res_out, mem_out, nrm_out, stab_out = pl.pallas_call(
+    results = pl.pallas_call(
         functools.partial(kernel, n, batch, heads, rows, dv, width, 1.0 / math.sqrt(rows * n)),
         out_shape=(
             pltpu.VMEM((batch, width), f32),
             pltpu.VMEM((batch, hr, dv), bf16),
             pltpu.VMEM(normalizer.shape, f32),
             pltpu.VMEM((heads, batch), f32),
+            pltpu.VMEM((n, batch, width), bf16),
+            pltpu.VMEM((groups, hr, GROUP), f32),
+            pltpu.VMEM((heads, groups, GROUP, LANES), f32),
         ),
         in_specs=[pl.BlockSpec(memory_space=pltpu.HBM)] * len(args),
-        out_specs=(pl.BlockSpec(memory_space=pltpu.VMEM),) * 4,
+        out_specs=(pl.BlockSpec(memory_space=pltpu.VMEM),) * 7,
         scratch_shapes=scratch,
         compiler_params=pltpu.CompilerParams(collective_id=0, has_side_effects=True, vmem_limit_bytes=40 * 1024 * 1024),
         name="mlstm_step",
     )(*args)
-    results = (res_out, mem_out, nrm_out, stab_out)
     res_out, mem_out, nrm_out, stab_out = pl.pallas_call(
         write_back,
-        out_shape=tuple(jax.ShapeDtypeStruct(a.shape, a.dtype) for a in results),
-        in_specs=[pl.BlockSpec(memory_space=pltpu.VMEM)] * 4,
+        out_shape=tuple(jax.ShapeDtypeStruct(a.shape, a.dtype) for a in results[:4]),
+        in_specs=[pl.BlockSpec(memory_space=pltpu.VMEM)] * 7,
         out_specs=(pl.BlockSpec(memory_space=pltpu.HBM),) * 4,
-        scratch_shapes=[dma((3 + PIECES,))],
-        compiler_params=pltpu.CompilerParams(vmem_limit_bytes=1024 * 1024),
+        scratch_shapes=[
+            pltpu.VMEM((batch, hr, dv), bf16),
+            pltpu.VMEM((n, groups, GROUP, width), f32),
+            dma((3 + groups,)),
+        ],
+        compiler_params=pltpu.CompilerParams(vmem_limit_bytes=12 * 1024 * 1024),
         name="write_back",
     )(*(pltpu.with_memory_space_constraint(a, pltpu.VMEM) for a in results))
     return res_out, mem_out.reshape(memory.shape), nrm_out, stab_out.T

time: 22.7 us -> 21.1 us (0.930)
  Pallas kernels: 21.9 us -> 20.4 us
    pallas_call x1, Pallas kernels: 19.2 us -> 17.5 us  [body(): pl.pallas_call(functools.partial(kernel, n, batch, heads, rows, dv, width...]
where the time goes in v2:
time: 21.1 us; the launch traced here: 21 us
  Pallas kernels  20.4 us (97%)
  between operations  0.64 us (3%)
    pallas_call x1, Pallas kernels, body(): pl.pallas_call(functools.partial(kernel, n, batch, heads, rows, dv, width...  17.5 us
    pallas_call x1, Pallas kernels, body(): pl.pallas_call(write_back, out_shape=tuple((jax.ShapeDtypeStruct(a.shape,...  2.8 us

profile of v2, /device:TPU:0, one launch (start us, length us, event | category | flops | bytes accessed | tf_op | source)
XLA Modules:
  0.0 21.0 jit_solution(5526650993737504714)
XLA Ops:
  0.6 17.5 %mlstm_step.1 = (f32[24,512]{1,0:T(8,128)S(1)}, bf16[24,256,512]{2,1,0:T(8,128)(2,1)S(1)}, f32[24,8,32]{2,1,0:T(8,128)S(1)}, f32[8,24]{1,0:T(8,128)S(1)}, bf16[8...) custom-call(f32[24,512]{1,0:T(8,128)} %res_hbm.1, f32[1,4096]{1,0:T(1,128)} %bitcast.12, ...), custom_call_target="tpu_custom_call" | custom-call | tf_op jit(solution)/shard_map/mlstm_step/pallas_call | solution.py:421
  18.2 2.8 %write_back.1 = (f32[24,512]{1,0:T(8,128)}, bf16[24,256,512]{2,1,0:T(8,128)(2,1)}, f32[24,8,32]{2,1,0:T(8,128)}, f32[8,24]{1,0:T(8,128)}) custom-call(f32[24,512]{1,0:T(8,128)S(1)} %get-tuple-element.15.res, bf16[24,256,512]{2,1,0:T(8,128)(2,1)S(1)} %get-tuple-element.16.mem, f32[24,8,32]{2,1,0:T(8,128)S(1)} %get-tuple-element.17.nrm, ...), custom_call_target="tpu_custom_call" | custom-call | tf_op jit(solution)/shard_map/write_back/pallas_call | solution.py:438

commit v3 on v2

--- a/solution.py
+++ b/solution.py
@@ -58,7 +58,7 @@
     res, gain, wq, wk, wv, wg, wi, wf, bi, bf, wo, nrm, stab,
     xs, sq, num_send, num_recv, den_send, den_recv, out_send, out_recv,
     kt_ref, qt_ref, n_rows, num_tile, val_rows,
-    in_sem, mem_sem, x_send, x_recv, sq_send, sq_recv, num_ss, num_rs, den_ss, den_rs, val_ss, val_rs, out_ss, out_rs,
+    in_sem, mem_sem, wide_ss, x_recv, sq_send, sq_recv, num_rs, den_ss, den_rs, val_rs, out_rs,
 ):
     me = lax.axis_index("head")
     groups = batch // GROUP
@@ -76,9 +76,9 @@
     source = peer
 
     def other(k):
-        return k + lax.div(k + n - me, n)
-
-    far_first = sorted(range(1, n), key=lambda d: (-(d >> 1).bit_count(), d % 2))
+        return n - k - lax.div(me + k, n) if k else lax.div(n - me, n)
+
+    far_first = sorted(range(1, n), key=lambda d: (-(d >> 1).bit_count(), 1 - d % 2, d))
 
     near = [d for d in far_first if d % 2 == 0] + [1]
     far = [d for d in far_first if d % 2 and d > 1]
@@ -129,19 +129,19 @@
     den_send[...] = jnp.zeros_like(den_send)
 
     def x_copy(d, owner):
-        return remote(xs.at[owner], xs.at[owner], x_send, x_recv.at[d - 1], peer(d))
+        return remote(xs.at[owner], xs.at[owner], wide_ss, x_recv.at[d - 1], peer(d))
 
     def sq_copy(d, owner):
         return remote(sq.at[owner], sq.at[owner], sq_send, sq_recv, peer(d))
 
     def val_copy(d, owner):
-        return remote(vals.at[owner], vals.at[owner], val_ss, val_rs.at[0 if d == 1 else 1 + d % 2], peer(d))
+        return remote(vals.at[owner], vals.at[owner], wide_ss, val_rs.at[0 if d == 1 else 1 + d % 2], peer(d))
 
     def val_relay(d):
-        return remote(vals.at[peer(d)], vals.at[peer(d)], val_ss, val_rs.at[2], peer(1))
+        return remote(vals.at[peer(d)], vals.at[peer(d)], wide_ss, val_rs.at[2], peer(1))
 
     def num_copy(d, g):
-        return remote(num_send.at[peer(d), g], num_recv.at[d - 1, g], num_ss, num_rs, peer(d))
+        return remote(num_send.at[peer(d), g], num_recv.at[d - 1, g], wide_ss, num_rs, peer(d))
 
     def den_copy(d):
         head = lax.div(peer(d) * width, share)
@@ -149,13 +149,13 @@
 
     def out_copy(k):
         target = other(k)
-        return remote(out_send.at[k], out_recv.at[lax.rem(me + n - target, n) - 1], out_ss, out_rs, target)
+        return remote(out_send.at[k], out_recv.at[lax.rem(me + n - target, n) - 1], wide_ss, out_rs, target)
 
     def whole(ref, ssem, rsem):
         return remote(ref, ref, ssem, rsem, peer(1))
 
     pl.semaphore_wait(barrier, n - 1)
-    for d in [1, 3, 5, 7, 2, 4, 6]:
+    for d in sorted(range(1, n), key=lambda d: (1 - d % 2, d)):
         x_copy(d, me).start()
     for d in far_first:
         sq_copy(d, me).start()
@@ -165,11 +165,10 @@
     l_nrm.wait()
     q_t = jnp.zeros((hr, batch), jnp.float32)
     k_t = jnp.zeros((hr, batch), jnp.float32)
-    for d in [0, 1, 3, 5, 2, 4, 7, 6]:
+    for d in sorted(range(n), key=lambda d: ((d >> 1).bit_count(), d > 0, 1 - d % 2, d)):
         owner = source(d)
         if d:
-            with jax.named_scope(f"qk{d}_wait"):
-                x_copy(d, owner).wait_recv()
+            x_copy(d, owner).wait_recv()
         cols = pl.ds(pl.multiple_of(owner * width, width), width)
         block = xs[owner]
         q_t += dot(wq[:, cols], block, NT)
@@ -268,18 +267,6 @@
     for d in near:
         val_copy(d, me).start()
 
-    key_t = kt_ref[...] * (s_row * key_scale)
-    for h in range(heads):
-        at = slice(h * rows, (h + 1) * rows)
-        ik = key_t[at, :] * i_gate[h : h + 1, :]
-        f_rows[h] = jnp.broadcast_to(to_col(f_gate[h : h + 1, :]), (batch, LANES)).reshape(groups, GROUP, LANES)
-        for g in range(groups):
-            kcols[g, at, :] = ik[:, g * GROUP : (g + 1) * GROUP]
-    for h in range(heads):
-        nrm_out[:, h, :] = to_col(f_gate[h : h + 1, :]) * nrm[:, h, :] + (
-            to_col(i_gate[h : h + 1, :]) * key[:, h * rows : (h + 1) * rows]
-        )
-
     my_head = lax.div(me * width, share)
     picked = lax.broadcasted_iota(jnp.int32, (heads, batch), 0) == my_head
 
@@ -300,7 +287,7 @@
     value_weight = to_col(i_row * kq_row / bound)
     l_wo.wait()
     numer = num_send[me].astype(jnp.float32)
-    all_num = whole(num_recv, num_ss, num_rs)
+    all_num = whole(num_recv, wide_ss, num_rs)
     all_num.wait_recv()
     for d in range(1, n):
         numer += num_recv[d - 1].astype(jnp.float32)
@@ -323,25 +310,36 @@
         for c in range(k, min(k + 2, n - 1)):
             out_copy(c).start()
     if n > 2:
-        whole(vals.at[pl.ds(0, n // 2 - 1)], val_ss, val_rs.at[1]).wait_recv()
+        whole(vals.at[pl.ds(0, n // 2 - 1)], wide_ss, val_rs.at[1]).wait_recv()
     for d in near[:-1]:
         val_relay(d).start()
+    key_t = kt_ref[...] * (s_row * key_scale)
+    for h in range(heads):
+        at = slice(h * rows, (h + 1) * rows)
+        ik = key_t[at, :] * i_gate[h : h + 1, :]
+        f_rows[h] = jnp.broadcast_to(to_col(f_gate[h : h + 1, :]), (batch, LANES)).reshape(groups, GROUP, LANES)
+        for g in range(groups):
+            kcols[g, at, :] = ik[:, g * GROUP : (g + 1) * GROUP]
+    for h in range(heads):
+        nrm_out[:, h, :] = to_col(f_gate[h : h + 1, :]) * nrm[:, h, :] + (
+            to_col(i_gate[h : h + 1, :]) * key[:, h * rows : (h + 1) * rows]
+        )
+
     val_copy(1, source(1)).wait_recv()
     if n > 2:
-        whole(vals.at[pl.ds(0, n // 2 - 1)], val_ss, val_rs.at[2]).wait_recv()
+        whole(vals.at[pl.ds(0, n // 2 - 1)], wide_ss, val_rs.at[2]).wait_recv()
     spread_values(vals, val_rows)
     for g in range(EARLY):
         update_group(mem, mem, val_rows, f_rows, kcols, g)
-    all_out = whole(out_recv, out_ss, out_rs)
+    all_out = whole(out_recv, wide_ss, out_rs)
     all_out.wait_recv()
     for d in range(1, n):
         branch += out_recv[d - 1].astype(jnp.float32)
     res_out[...] = res[...] + branch
 
-    whole(xs.at[pl.ds(0, n - 1)], x_send, x_recv.at[0]).wait_send()
-    whole(vals.at[pl.ds(0, n - 1)], val_ss, val_rs.at[0]).wait_send()
-    for copy in (all_sq, all_num, all_den, all_out):
-        copy.wait_send()
+    whole(wv.at[pl.ds(0, 4 * (n - 1) * batch)], wide_ss, out_rs).wait_send()
+    all_sq.wait_send()
+    all_den.wait_send()
 
 def write_back(res, mem, nrm, stab, vals, kcols, f_rows, res_out, mem_out, nrm_out, stab_out, staged, val_rows, sem):
     groups = mem.shape[0] // GROUP
@@ -414,9 +412,8 @@
         dma((13,)),
         dma((groups,)),
         dma, dma((n - 1,)),
-        dma, dma, dma, dma, dma, dma,
-        dma, dma((3,)),
-        dma, dma,
+        dma, dma, dma, dma, dma,
+        dma((3,)), dma,
     ]
     results = pl.pallas_call(
         functools.partial(kernel, n, batch, heads, rows, dv, width, 1.0 / math.sqrt(rows * n)),

time: 21.1 us -> 20.9 us (level)
  Pallas kernels: 20.4 us -> 20 us
    pallas_call x1, Pallas kernels: 17.5 us -> 17.2 us  [body(): pl.pallas_call(functools.partial(kernel, n, batch, heads, rows, dv, width...]
where the time goes in v3:
time: 20.9 us; the launch traced here: 20.6 us
  Pallas kernels  20 us (96%)
  between operations  0.64 us (3%)
    pallas_call x1, Pallas kernels, body(): pl.pallas_call(functools.partial(kernel, n, batch, heads, rows, dv, width...  17.2 us
    pallas_call x1, Pallas kernels, body(): pl.pallas_call(write_back, out_shape=tuple((jax.ShapeDtypeStruct(a.shape,...  2.8 us

profile of v3, /device:TPU:0, one launch (start us, length us, event | category | flops | bytes accessed | tf_op | source)
XLA Modules:
  0.0 20.6 jit_solution(6105183959096292654)
XLA Ops:
  0.6 17.2 %mlstm_step.1 = (f32[24,512]{1,0:T(8,128)S(1)}, bf16[24,256,512]{2,1,0:T(8,128)(2,1)S(1)}, f32[24,8,32]{2,1,0:T(8,128)S(1)}, f32[8,24]{1,0:T(8,128)S(1)}, bf16[8...) custom-call(f32[24,512]{1,0:T(8,128)} %res_hbm.1, f32[1,4096]{1,0:T(1,128)} %bitcast.12, ...), custom_call_target="tpu_custom_call" | custom-call | tf_op jit(solution)/shard_map/mlstm_step/pallas_call | solution.py:418
  17.8 2.8 %write_back.1 = (f32[24,512]{1,0:T(8,128)}, bf16[24,256,512]{2,1,0:T(8,128)(2,1)}, f32[24,8,32]{2,1,0:T(8,128)}, f32[8,24]{1,0:T(8,128)}) custom-call(f32[24,512]{1,0:T(8,128)S(1)} %get-tuple-element.15.res, bf16[24,256,512]{2,1,0:T(8,128)(2,1)S(1)} %get-tuple-element.16.mem, f32[24,8,32]{2,1,0:T(8,128)S(1)} %get-tuple-element.17.nrm, ...), custom_call_target="tpu_custom_call" | custom-call | tf_op jit(solution)/shard_map/write_back/pallas_call | solution.py:435
